TPU v7x, 32 devices: a whole 2x2x4 slice. The times are simulated.
32 devices in a mesh: blk: 8 (over y, x, core), uly: 4 (over z).
Axes of the slice: x: 2, y: 2, z: 4, core: 2. Of those that a mesh axis runs over, the one named last changes fastest.
Arguments:
- queries: bfloat16 [4096, 4096], P(('blk', 'uly')), may hold values from -128 to 128
- keys: bfloat16 [4096, 1024], P(('blk', 'uly')), may hold values from -7 to 7
- values: bfloat16 [4096, 1024], P(('blk', 'uly')), may hold values from -6 to 6
- doc_ids: int32 [4096], P(('blk', 'uly')), may hold values from 0 to 31, never falling along the last dimension, each value on 1 to 512 neighbouring positions
- out_weight: bfloat16 [4096, 4096], P('uly'), may hold values from -0.09375 to 0.09375
Outputs:
- mixed: bfloat16 [4096, 4096], P(('blk', 'uly'))
Inputs may be any that keep to these rules, and one draw needn't show every extreme that they name: `doc_ids`: document numbers never fall along the pack; each document holds 1 to 512 consecutive tokens, and some document holds exactly 512.
All inputs are finite; a program needn't handle non-finite values.
Results may differ from a plain program's by a relative error of at most 0.017.
Values may be sent and summed in bfloat16 or wider, within the bound.
A program may use at most 64 MiB of HBM per device.

v0:
```python
import math
import jax
import jax.numpy as jnp
from jax import lax
from jax.sharding import PartitionSpec as P

HEAD_DIM = 128


def shifted(value, axis, steps):
    count = lax.axis_size(axis)
    first, last = (max(0, -steps), min(count, count - steps))
    return lax.ppermute(value, axis, [(source, source + steps) for source in range(first, last)])


def body(queries, keys, values, doc_ids, out_weight):
    n_uly = lax.axis_size("uly")
    blk_index = lax.axis_index("blk")
    rows = queries.shape[0]
    head_dim = HEAD_DIM
    heads = queries.shape[1] // head_dim
    kv_heads = keys.shape[1] // head_dim
    repeat = max(1, n_uly // kv_heads)
    kv_local = max(n_uly, kv_heads) // n_uly
    local_heads = heads // n_uly
    grouped = local_heads // kv_local
    block = rows * n_uly
    sub_rows = math.gcd(block, 512)
    n_sub = block // sub_rows
    scale = 1.0 / math.sqrt(head_dim)
    query_ids = lax.all_gather(doc_ids, "uly", axis=0, tiled=True)
    query_split = queries.reshape(rows, heads, head_dim)
    key_wide = jnp.repeat(keys.reshape(rows, kv_heads, head_dim), repeat, axis=1)
    value_wide = jnp.repeat(values.reshape(rows, kv_heads, head_dim), repeat, axis=1)
    key_wide, value_wide = (key_wide, value_wide)
    query_local, key_local, value_local = (
        lax.all_to_all(query_split, "uly", split_axis=1, concat_axis=0, tiled=True),
        lax.all_to_all(key_wide, "uly", split_axis=1, concat_axis=0, tiled=True),
        lax.all_to_all(value_wide, "uly", split_axis=1, concat_axis=0, tiled=True),
    )
    carried = (key_local, value_local)
    query_grouped = query_local.reshape(n_sub, sub_rows, kv_local, grouped, head_dim)
    query_start = blk_index * block
    query_pos = query_start + jnp.arange(block, dtype=jnp.int32)
    first_id = query_ids[0]
    offsets = jnp.arange(block, dtype=jnp.int32)
    ids_sub = query_ids.reshape(n_sub, sub_rows)
    pos_sub = query_pos.reshape(n_sub, sub_rows)

    def attend(state, pair, key_ids, source):
        key_block, value_block = pair
        key_start = jnp.maximum(source, 0) * block
        key_pos = key_start + offsets
        needed = (source >= 0) & (
            (source == blk_index) | (source < blk_index) & (key_ids[block - 1] == first_id)
        )

        def compute(state_in):

            def one(item):
                query_part, pos_part, ids_part, accum, peak, total = item
                scores = (
                    jnp.einsum(
                        "qkgd,pkd->kgqp", query_part, key_block, preferred_element_type=jnp.float32
                    )
                    * scale
                )
                allowed = (key_pos[None, :] <= pos_part[:, None]) & (
                    key_ids[None, :] == ids_part[:, None]
                )
                scores = jnp.where(allowed, scores, -1e30)
                peak_new = jnp.maximum(peak, jnp.max(scores, axis=-1))
                expo = jnp.where(allowed, jnp.exp(scores - peak_new[..., None]), 0.0)
                factor = jnp.exp(peak - peak_new)
                total_new = total * factor + jnp.sum(expo, axis=-1)
                update = jnp.einsum(
                    "kgqp,pkd->kgqd",
                    expo.astype(jnp.bfloat16),
                    value_block,
                    preferred_element_type=jnp.float32,
                )
                return (accum * factor[..., None] + update, peak_new, total_new)

            return lax.map(
                one, (query_grouped, pos_sub, ids_sub, state_in[0], state_in[1], state_in[2])
            )

        def keep(state_in):
            return state_in

        return lax.cond(needed, compute, keep, state)

    start_state = (
        jnp.zeros((n_sub, kv_local, grouped, sub_rows, head_dim), jnp.float32),
        jnp.full((n_sub, kv_local, grouped, sub_rows), -1e30, jnp.float32),
        jnp.zeros((n_sub, kv_local, grouped, sub_rows), jnp.float32),
    )
    state = attend(start_state, carried, query_ids, blk_index)
    earlier_key, earlier_value, earlier_marks = shifted(
        (carried[0], carried[1], query_ids.astype(jnp.bfloat16)), "blk", 1
    )
    earlier_ids = earlier_marks.astype(jnp.int32)
    state = attend(state, (earlier_key, earlier_value), earlier_ids, blk_index - 1)
    accum, peak, total = state
    attn = (
        (accum / total[..., None])
        .transpose(0, 3, 1, 2, 4)
        .reshape(block, local_heads * head_dim)
        .astype(jnp.bfloat16)
    )
    mixed = lax.psum_scatter(
        jnp.dot(attn, out_weight, preferred_element_type=jnp.float32).astype(jnp.bfloat16),
        "uly",
        scatter_dimension=0,
        tiled=True,
    )
    return mixed


def solution(mesh):
    placed = (
        P(("blk", "uly"), None),
        P(("blk", "uly"), None),
        P(("blk", "uly"), None),
        P(("blk", "uly")),
        P("uly", None),
    )
    return jax.shard_map(
        body, mesh=mesh, in_specs=placed, out_specs=P(("blk", "uly"), None), check_vma=False
    )
```

profile of v0, /device:TPU:0, one launch (start us, length us, event | category | flops | bytes accessed | tf_op | source)
XLA Modules:
  0.0 184.7 jit_solution(14577532152778803910)
XLA Ops:
  6.5 1.8 copy.38
  8.3 6.3 %all-to-all-start.1 = ((bf16[128,8,128]{0,2,1:T(8,128)(2,1)}), bf16[128,8,128]{0,2,1:T(8,128)(2,1)S(1)}, u32[]{:S(2)}, u32[]{:S(2)}) async-start(bf16[128,8,128]{0,2,1:T(8,128)(2,1)} %bitcast.33), calls=%async_computation.1 | async-start | bytes 524288 | tf_op jit(solution)/shard_map/all_to_all | solution.py:38
  14.7 1.8 copy.41
  16.5 7.1 %all-to-all-done.1 = bf16[128,8,128]{0,2,1:T(8,128)(2,1)S(1)} async-done(((bf16[128,8,128]{0,2,1:T(8,128)(2,1)}), bf16[128,8,128]{0,2,1:T(8,128)(2,1)S(1)}, u32[]{:S(2)}, u32[]{:S(2)}) %all-to-all-start.1) | async-done | bytes 262176 | tf_op jit(solution)/shard_map/all_to_all | solution.py:38
  23.6 3.4 %all-to-all-start.2 = ((bf16[128,8,128]{0,2,1:T(8,128)(2,1)}), bf16[128,8,128]{0,2,1:T(8,128)(2,1)S(1)}, u32[]{:S(2)}, u32[]{:S(2)}) async-start(bf16[128,8,128]{0,2,1:T(8,128)(2,1)} %bitcast.38), calls=%async_computation.2 | async-start | bytes 524288 | tf_op jit(solution)/shard_map/all_to_all | solution.py:39
  27.0 1.6 copy.34
  28.6 1.3 copy.35
  29.9 4.1 %all-to-all-done.2 = bf16[128,8,128]{0,2,1:T(8,128)(2,1)S(1)} async-done(((bf16[128,8,128]{0,2,1:T(8,128)(2,1)}), bf16[128,8,128]{0,2,1:T(8,128)(2,1)S(1)}, u32[]{:S(2)}, u32[]{:S(2)}) %all-to-all-start.2) | async-done | bytes 262176 | tf_op jit(solution)/shard_map/all_to_all | solution.py:39
  34.0 3.5 %all-to-all-start = ((bf16[128,32,128]{2,0,1:T(8,128)(2,1)}), bf16[128,32,128]{2,0,1:T(8,128)(2,1)S(1)}, u32[]{:S(2)}, u32[]{:S(2)}) async-start(bf16[128,32,128]{2,0,1:T(8,128)(2,1)} %copy.35), calls=%async_computation | async-start | bytes 2097152 | tf_op jit(solution)/shard_map/all_to_all | solution.py:37
  37.6 0.8 copy.40
  38.4 0.9 copy.43
  39.3 1.3 collective-permute-start.1
  40.6 4.8 %collective-permute-start.2 = (bf16[512,2,128]{2,0,1:T(8,128)(2,1)}, bf16[512,2,128]{2,0,1:T(8,128)(2,1)}, u32[]{:S(2)}, u32[]{:S(2)}) collective-permute-start(bf16[512,2,128]{2,0,1:T(8,128)(2,1)} %bitcast.42), channel_id=1, source_target_pairs={{0,4},{4,8},{8,12},{12,16},{16,20},{20,24},{24,28},{1,5},{5,9},{9,... | collective-permute-start | bytes 786440 | tf_op jit(solution)/shard_map/ppermute | solution.py:13
  45.4 12.3 %all-gather = s32[4,1,128]{2,1,0:T(1,128)S(1)} all-gather(s32[1,1,128]{2,1,0:T(1,128)S(1)} %bitcast.133), channel_id=1, replica_groups=mesh['blk'=8,'uly'=4] {'uly'}, dimensions={0}, use_global_device_ids=true | all-gather | bytes 2560 | tf_op jit(solution)/shard_map/all_gather | solution.py:31
  57.7 1.3 collective-permute-start
  61.8 8.8 %conditional.2 = (f32[1,2,4,512,128]{4,3,2,1,0:T(8,128)S(1)}, f32[1,2,4,512]{3,2,1,0:T(4,128)S(1)}, f32[1,2,4,512]{3,2,1,0:T(4,128)S(1)}) conditional(s32[]{:T(128)} %convert_element_type.35, () %tuple.24, (s32[]{:T(128)}, s32[512]{0:T(512)S(1)}, s32[1,512]{1,0:T(1,128)S(1)}, s32[512]{0:T(512)S(1)}, s32[1,512]{1,0:T(1,128)S(1)}, ...), branch_computations={%region_0.0_spmd, %region_1.4_spmd} | conditional | flops 1102336512 | bytes 30093364 | solution.py:91
  62.1 2.5 %fusion = (f32[2,4,512]{2,1,0:T(4,128)S(1)}, f32[2,512,512,4]{2,1,3,0:T(8,128)S(1)}) fusion(pred[512,512]{0,1:T(8,128)(4,1)S(1)} %compare_and_fusion, bf16[1,512,2,4,128]{4,1,3,2,0:T(8,128)(2,1)S(1)} %get-tuple-element.136, bf16[512,2,128]{2,0,1:T(8,128)(2,1)} %get-tuple-element.134), kind=kOutput, calls=%fused_computation.2 | convolution fusion | flops 543158272 | bytes 9977856 | tf_op jit(solution)/shard_map/cond/branch_1_fun/while/body/eval_jaxpr/qkgd,pkd->kgqp/dot_general | solution.py:63
  64.6 3.9 %add_bitcast_fusion = f32[1,2,4,512,128]{4,3,2,1,0:T(8,128)S(1)} fusion(f32[2,512,512,4]{2,1,3,0:T(8,128)S(1)} %get-tuple-element.172, f32[2,4,512]{2,1,0:T(4,128)S(1)} %get-tuple-element.170, pred[512,512]{0,1:T(8,128)(4,1)S(1)} %compare_and_fusion, f32[2,4,512]{2,1,0:T(4,128)S(1)} %get-tuple-element.169, bf16[512,2,128]{2,0,1:T(8,128)(2,1)} %get-tuple-element.138), kind=kOutput, calls=%fused_computation.7 | convolution fusion | flops 547880960 | bytes 11042816 | tf_op jit(solution)/shard_map/cond/branch_1_fun/while/body/eval_jaxpr/kgqp,pkd->kgqd/dot_general | solution.py:76
  68.5 2.0 %fusion.1 = f32[2,4,512]{2,1,0:T(4,128)S(1)} fusion(f32[2,512,512,4]{2,1,3,0:T(8,128)S(1)} %get-tuple-element.172, f32[2,4,512]{2,1,0:T(4,128)S(1)} %get-tuple-element.170, pred[512,512]{0,1:T(8,128)(4,1)S(1)} %compare_and_fusion), kind=kLoop, calls=%fused_computation.3 | loop fusion | flops 10481664 | bytes 8683520 | tf_op jit(solution)/shard_map/cond/branch_1_fun/while/body/eval_jaxpr/reduce_sum | solution.py:75
  70.6 1.8 conditional.3
  70.6 1.8 copy.54
  72.4 1.9 %divide_convert_fusion = bf16[1,2,4,512,128]{3,4,2,1,0:T(8,128)(2,1)S(1)} fusion(f32[1,2,4,512,128]{3,4,2,1,0:T(8,128)} %get-tuple-element.162, f32[2,4,512]{2,1,0:T(4,128)S(1)} %bitcast.122), kind=kLoop, calls=%fused_computation.48 | loop fusion | flops 1048576 | bytes 3162112 | tf_op jit(solution)/shard_map/convert_element_type | solution.py:109
  74.3 9.5 %convolution_convert_fusion = bf16[512,4096]{1,0:T(8,128)(2,1)} fusion(bf16[512,1024]{0,1:T(8,128)(2,1)S(1)} %bitcast.119, bf16[1024,4096]{1,0:T(8,128)(2,1)} %param.13), kind=kOutput, calls=%fused_computation.47 | convolution fusion | flops 4297064448 | bytes 13631488 | tf_op jit(solution)/shard_map/dot_general | solution.py:112
  83.8 94.0 %reduce-scatter.2.cloned.1.call-done = bf16[128,4096]{1,0:T(8,128)(2,1)} async-done(((bf16[512,4096]{1,0:T(8,128)(2,1)}), bf16[128,4096]{1,0:T(8,128)(2,1)}) %reduce-scatter.2.cloned.1.call-update) | async-done | bytes 1048592 | tf_op jit(solution)/shard_map/reduce_scatter | solution.py:111
  (20 shorter events, 1.9 us)
Async XLA Ops:
  6.5 38.9 %copy-start = (s32[128]{0:T(128)S(1)}, s32[128]{0:T(128)}, u32[]{:S(2)}) copy-start(s32[128]{0:T(128)} %param.12) | copy-start | bytes 1540
  8.3 15.3 %all-to-all-start.1 = ((bf16[128,8,128]{0,2,1:T(8,128)(2,1)}), bf16[128,8,128]{0,2,1:T(8,128)(2,1)S(1)}, u32[]{:S(2)}, u32[]{:S(2)}) async-start(bf16[128,8,128]{0,2,1:T(8,128)(2,1)} %bitcast.33), calls=%async_computation.1 | async-start | bytes 524288 | tf_op jit(solution)/shard_map/all_to_all | solution.py:38
  23.6 10.4 %all-to-all-start.2 = ((bf16[128,8,128]{0,2,1:T(8,128)(2,1)}), bf16[128,8,128]{0,2,1:T(8,128)(2,1)S(1)}, u32[]{:S(2)}, u32[]{:S(2)}) async-start(bf16[128,8,128]{0,2,1:T(8,128)(2,1)} %bitcast.38), calls=%async_computation.2 | async-start | bytes 524288 | tf_op jit(solution)/shard_map/all_to_all | solution.py:39
  34.0 27.6 %all-to-all-start = ((bf16[128,32,128]{2,0,1:T(8,128)(2,1)}), bf16[128,32,128]{2,0,1:T(8,128)(2,1)S(1)}, u32[]{:S(2)}, u32[]{:S(2)}) async-start(bf16[128,32,128]{2,0,1:T(8,128)(2,1)} %copy.35), calls=%async_computation | async-start | bytes 2097152 | tf_op jit(solution)/shard_map/all_to_all | solution.py:37
  37.5 140.3 %reduce-scatter.2.cloned.1.call-start = ((), (), s32[]{:S(2)}) async-start(), calls=%async_computation.4 | async-start | bytes 5242880 | tf_op jit(solution)/shard_map/reduce_scatter | solution.py:111
  39.3 31.3 %collective-permute-start.1 = (bf16[512,2,128]{2,0,1:T(8,128)(2,1)}, bf16[512,2,128]{2,0,1:T(8,128)(2,1)S(1)}, u32[]{:S(2)}, u32[]{:S(2)}) collective-permute-start(bf16[512,2,128]{2,0,1:T(8,128)(2,1)} %bitcast.37), channel_id=1, source_target_pairs={{0,4},{4,8},{8,12},{12,16},{16,20},{20,24},{24,28},{1,5},{5,9},{9,... | collective-permute-start | bytes 786440 | tf_op jit(solution)/shard_map/ppermute | solution.py:13
  40.6 30.0 %collective-permute-start.2 = (bf16[512,2,128]{2,0,1:T(8,128)(2,1)}, bf16[512,2,128]{2,0,1:T(8,128)(2,1)}, u32[]{:S(2)}, u32[]{:S(2)}) collective-permute-start(bf16[512,2,128]{2,0,1:T(8,128)(2,1)} %bitcast.42), channel_id=1, source_target_pairs={{0,4},{4,8},{8,12},{12,16},{16,20},{20,24},{24,28},{1,5},{5,9},{9,... | collective-permute-start | bytes 786440 | tf_op jit(solution)/shard_map/ppermute | solution.py:13
  57.7 2.1 %collective-permute-start = (bf16[512]{0:T(512)(128)(2,1)S(1)}, bf16[512]{0:T(512)(128)(2,1)S(1)}, u32[]{:S(2)}, u32[]{:S(2)}) collective-permute-start(bf16[512]{0:T(512)(128)(2,1)S(1)} %convert_element_type.32), channel_id=1, source_target_pairs={{0,4},{4,8},{8,12},{12,16},{16,20},{20,24},{24,28},{1,5},{5,9},{9,... | collective-permute-start | bytes 3080 | tf_op jit(solution)/shard_map/ppermute | solution.py:13
Sparse Core Ops, SparseCore 0:
  84.0 93.8 reduce-scatter.1
where the time goes:
time: 185 us
  waiting for transfers between devices  106 us (57%)
  starting transfers between devices  20.7 us (11%)
  matrix products  15.9 us (9%)
  between operations  14.8 us (8%)
  blocking collectives  12.3 us (7%)
  local copies, waits for them, and re-layouts  11.3 us (6%)
  other arithmetic  4.25 us (2%)
    reduce_scatter x1, waiting for transfers between devices, body(): lax.psum_scatter(jnp.dot(attn, out_weight, preferred_element_type=jnp.flo...  94 us
    all_gather x1, blocking collectives, body(): query_ids = lax.all_gather(doc_ids, 'uly', axis=0, tiled=True)  12.3 us
    dot_general x1, matrix products, body(): jnp.dot(attn, out_weight, preferred_element_type=jnp.float32)  9.49 us
    ppermute x3, starting transfers between devices, shifted(): lax.ppermute(value, axis, [(source, source + steps) for source in range(f...  7.39 us
    all_to_all x1, waiting for transfers between devices, body(): lax.all_to_all(key_wide, 'uly', split_axis=1, concat_axis=0, tiled=True)  7.13 us
    all_to_all x1, starting transfers between devices, body(): lax.all_to_all(key_wide, 'uly', split_axis=1, concat_axis=0, tiled=True)  6.35 us
    unnamed x5, local copies, waits for them, and re-layouts  5.2 us
    all_to_all x1, waiting for transfers between devices, body(): lax.all_to_all(value_wide, 'uly', split_axis=1, concat_axis=0, tiled=True)  4.06 us
  transfers between devices with their start and end apart: 7, of which 4 were waited for; matrix products, arithmetic and copies ran while one was open for 9% of the time, Pallas kernels for 0%

commit v1 on v0

--- a/solution.py
+++ b/solution.py
@@ -28,7 +28,12 @@
     sub_rows = math.gcd(block, 512)
     n_sub = block // sub_rows
     scale = 1.0 / math.sqrt(head_dim)
-    query_ids = lax.all_gather(doc_ids, "uly", axis=0, tiled=True)
+    ring = [doc_ids]
+    for hop in range(3):
+        ring.append(lax.ppermute(ring[-1], "uly", [(dev, (dev + 1) % 4) for dev in range(4)]))
+    query_ids = jnp.roll(
+        jnp.concatenate(ring[::-1], axis=0), (lax.axis_index("uly") + 1) * ring[0].shape[0], axis=0
+    )
     query_split = queries.reshape(rows, heads, head_dim)
     key_wide = jnp.repeat(keys.reshape(rows, kv_heads, head_dim), repeat, axis=1)
     value_wide = jnp.repeat(values.reshape(rows, kv_heads, head_dim), repeat, axis=1)

time: 185 us -> 197 us (1.065)
  waiting for transfers between devices: 106 us -> 123 us
  blocking collectives: 12.3 us -> 0 us
  starting transfers between devices: 20.7 us -> 27.5 us
    ppermute x0 -> x3, waiting for transfers between devices: none -> 22.3 us  [body(): lax.ppermute(ring[-1], 'uly', [(dev, (dev + 1) % 4) for dev in range(4)])]
    all_gather x1 -> x0, blocking collectives: 12.3 us -> none  [body(): query_ids = lax.all_gather(doc_ids, 'uly', axis=0, tiled=True)]
    ppermute x0 -> x3, starting transfers between devices: none -> 6.79 us  [body(): lax.ppermute(ring[-1], 'uly', [(dev, (dev + 1) % 4) for dev in range(4)])]
    reduce_scatter x1, waiting for transfers between devices: 94 us -> 88.9 us  [body(): lax.psum_scatter(jnp.dot(attn, out_weight, preferred_element_type=jnp.flo...]
    unnamed x5 -> x12, local copies, waits for them, and re-layouts: 5.2 us -> 5.26 us
  transfers between devices with their start and end apart: 7 -> 10, of which waited for: 4 -> 7; matrix products, arithmetic and copies ran while one was open for 9% -> 8% of each run, Pallas kernels for 0% -> 0%
where the time goes in v1:
time: 197 us
  waiting for transfers between devices  123 us (62%)
  starting transfers between devices  27.5 us (14%)
  matrix products  15.9 us (8%)
  between operations  14.8 us (8%)
  local copies, waits for them, and re-layouts  11.4 us (6%)
  other arithmetic  4.33 us (2%)
    reduce_scatter x1, waiting for transfers between devices, body(): lax.psum_scatter(jnp.dot(attn, out_weight, preferred_element_type=jnp.flo...  88.9 us
    ppermute x3, waiting for transfers between devices, body(): lax.ppermute(ring[-1], 'uly', [(dev, (dev + 1) % 4) for dev in range(4)])  22.3 us
    dot_general x1, matrix products, body(): jnp.dot(attn, out_weight, preferred_element_type=jnp.float32)  9.5 us
    ppermute x3, starting transfers between devices, shifted(): lax.ppermute(value, axis, [(source, source + steps) for source in range(f...  7.39 us
    all_to_all x1, waiting for transfers between devices, body(): lax.all_to_all(key_wide, 'uly', split_axis=1, concat_axis=0, tiled=True)  7.12 us
    ppermute x3, starting transfers between devices, body(): lax.ppermute(ring[-1], 'uly', [(dev, (dev + 1) % 4) for dev in range(4)])  6.79 us
    all_to_all x1, starting transfers between devices, body(): lax.all_to_all(key_wide, 'uly', split_axis=1, concat_axis=0, tiled=True)  6.35 us
    unnamed x12, local copies, waits for them, and re-layouts  5.26 us
  transfers between devices with their start and end apart: 10, of which 7 were waited for; matrix products, arithmetic and copies ran while one was open for 8% of the time, Pallas kernels for 0%

profile of v1, /device:TPU:0, one launch (start us, length us, event | category | flops | bytes accessed | tf_op | source)
XLA Modules:
  0.0 196.5 jit_solution(5128243767702903765)
XLA Ops:
  6.5 1.8 copy.38
  8.3 6.3 %all-to-all-start.1 = ((bf16[128,8,128]{0,2,1:T(8,128)(2,1)}), bf16[128,8,128]{0,2,1:T(8,128)(2,1)S(1)}, u32[]{:S(2)}, u32[]{:S(2)}) async-start(bf16[128,8,128]{0,2,1:T(8,128)(2,1)} %bitcast.31), calls=%async_computation.1 | async-start | bytes 524288 | tf_op jit(solution)/shard_map/all_to_all | solution.py:43
  14.7 1.8 copy.41
  16.5 7.1 %all-to-all-done.1 = bf16[128,8,128]{0,2,1:T(8,128)(2,1)S(1)} async-done(((bf16[128,8,128]{0,2,1:T(8,128)(2,1)}), bf16[128,8,128]{0,2,1:T(8,128)(2,1)S(1)}, u32[]{:S(2)}, u32[]{:S(2)}) %all-to-all-start.1) | async-done | bytes 262176 | tf_op jit(solution)/shard_map/all_to_all | solution.py:43
  23.6 3.4 %all-to-all-start.2 = ((bf16[128,8,128]{0,2,1:T(8,128)(2,1)}), bf16[128,8,128]{0,2,1:T(8,128)(2,1)S(1)}, u32[]{:S(2)}, u32[]{:S(2)}) async-start(bf16[128,8,128]{0,2,1:T(8,128)(2,1)} %bitcast.36), calls=%async_computation.2 | async-start | bytes 524288 | tf_op jit(solution)/shard_map/all_to_all | solution.py:44
  27.0 1.6 copy.34
  29.9 4.1 %all-to-all-done.2 = bf16[128,8,128]{0,2,1:T(8,128)(2,1)S(1)} async-done(((bf16[128,8,128]{0,2,1:T(8,128)(2,1)}), bf16[128,8,128]{0,2,1:T(8,128)(2,1)S(1)}, u32[]{:S(2)}, u32[]{:S(2)}) %all-to-all-start.2) | async-done | bytes 262176 | tf_op jit(solution)/shard_map/all_to_all | solution.py:44
  34.0 3.5 %all-to-all-start = ((bf16[128,32,128]{2,0,1:T(8,128)(2,1)}), bf16[128,32,128]{2,0,1:T(8,128)(2,1)S(1)}, u32[]{:S(2)}, u32[]{:S(2)}) async-start(bf16[128,32,128]{2,0,1:T(8,128)(2,1)} %copy.35), calls=%async_computation | async-start | bytes 2097152 | tf_op jit(solution)/shard_map/all_to_all | solution.py:42
  37.6 1.9 collective-permute-start
  39.5 16.5 %collective-permute-done = s32[128]{0:T(128)S(1)} collective-permute-done((s32[128]{0:T(128)S(1)}, s32[128]{0:T(128)S(1)}, u32[]{:S(2)}, u32[]{:S(2)}) %collective-permute-start) | collective-permute-done | bytes 544 | tf_op jit(solution)/shard_map/ppermute | solution.py:33
  56.0 3.3 %collective-permute-start.1 = (s32[128]{0:T(128)S(1)}, s32[128]{0:T(128)S(1)}, u32[]{:S(2)}, u32[]{:S(2)}) collective-permute-start(s32[128]{0:T(128)S(1)} %collective-permute-done), channel_id=1, source_target_pairs={{0,1},{1,2},{2,3},{3,0},{4,5},{5,6},{6,7},{7,4},{8,9},{9,10},{10,1... | collective-permute-start | bytes 1544 | tf_op jit(solution)/shard_map/ppermute | solution.py:33
  59.3 2.1 %collective-permute-done.1 = s32[128]{0:T(128)S(1)} collective-permute-done((s32[128]{0:T(128)S(1)}, s32[128]{0:T(128)S(1)}, u32[]{:S(2)}, u32[]{:S(2)}) %collective-permute-start.1) | collective-permute-done | bytes 544 | tf_op jit(solution)/shard_map/ppermute | solution.py:33
  61.3 1.6 collective-permute-start.2
  62.9 3.8 %collective-permute-done.2 = s32[128]{0:T(128)S(1)} collective-permute-done((s32[128]{0:T(128)S(1)}, s32[128]{0:T(128)S(1)}, u32[]{:S(2)}, u32[]{:S(2)}) %collective-permute-start.2) | collective-permute-done | bytes 544 | tf_op jit(solution)/shard_map/ppermute | solution.py:33
  69.8 4.8 %collective-permute-start.5 = (bf16[512,2,128]{2,0,1:T(8,128)(2,1)}, bf16[512,2,128]{2,0,1:T(8,128)(2,1)}, u32[]{:S(2)}, u32[]{:S(2)}) collective-permute-start(bf16[512,2,128]{2,0,1:T(8,128)(2,1)} %bitcast.40), channel_id=1, source_target_pairs={{0,4},{4,8},{8,12},{12,16},{16,20},{20,24},{24,28},{1,5},{5,9},{9,... | collective-permute-start | bytes 786440 | tf_op jit(solution)/shard_map/ppermute | solution.py:13
  78.7 8.8 %conditional.2 = (f32[1,2,4,512,128]{4,3,2,1,0:T(8,128)S(1)}, f32[1,2,4,512]{3,2,1,0:T(4,128)S(1)}, f32[1,2,4,512]{3,2,1,0:T(4,128)S(1)}) conditional(s32[]{:T(128)} %convert_element_type.35, () %tuple.24, (s32[]{:T(128)}, s32[512]{0:T(512)S(1)}, s32[1,512]{1,0:T(1,128)S(1)}, s32[512]{0:T(512)S(1)}, s32[1,512]{1,0:T(1,128)S(1)}, ...), branch_computations={%region_0.1_spmd, %region_1.4_spmd} | conditional | flops 1102336512 | bytes 30093364 | solution.py:96
  79.0 2.5 %fusion = (f32[2,4,512]{2,1,0:T(4,128)S(1)}, f32[2,512,512,4]{2,1,3,0:T(8,128)S(1)}) fusion(pred[512,512]{0,1:T(8,128)(4,1)S(1)} %compare_and_fusion, bf16[1,512,2,4,128]{4,1,3,2,0:T(8,128)(2,1)S(1)} %get-tuple-element.136, bf16[512,2,128]{2,0,1:T(8,128)(2,1)} %get-tuple-element.134), kind=kOutput, calls=%fused_computation.2 | convolution fusion | flops 543158272 | bytes 9977856 | tf_op jit(solution)/shard_map/cond/branch_1_fun/while/body/eval_jaxpr/qkgd,pkd->kgqp/dot_general | solution.py:68
  81.5 3.9 %add_bitcast_fusion = f32[1,2,4,512,128]{4,3,2,1,0:T(8,128)S(1)} fusion(f32[2,512,512,4]{2,1,3,0:T(8,128)S(1)} %get-tuple-element.174, f32[2,4,512]{2,1,0:T(4,128)S(1)} %get-tuple-element.172, pred[512,512]{0,1:T(8,128)(4,1)S(1)} %compare_and_fusion, f32[2,4,512]{2,1,0:T(4,128)S(1)} %get-tuple-element.171, bf16[512,2,128]{2,0,1:T(8,128)(2,1)} %get-tuple-element.138), kind=kOutput, calls=%fused_computation.7 | convolution fusion | flops 547880960 | bytes 11042816 | tf_op jit(solution)/shard_map/cond/branch_1_fun/while/body/eval_jaxpr/kgqp,pkd->kgqd/dot_general | solution.py:81
  85.4 2.0 %fusion.1 = f32[2,4,512]{2,1,0:T(4,128)S(1)} fusion(f32[2,512,512,4]{2,1,3,0:T(8,128)S(1)} %get-tuple-element.174, f32[2,4,512]{2,1,0:T(4,128)S(1)} %get-tuple-element.172, pred[512,512]{0,1:T(8,128)(4,1)S(1)} %compare_and_fusion), kind=kLoop, calls=%fused_computation.3 | loop fusion | flops 10481664 | bytes 8683520 | tf_op jit(solution)/shard_map/cond/branch_1_fun/while/body/eval_jaxpr/reduce_sum | solution.py:80
  87.5 1.9 conditional.3
  87.6 1.8 copy.54
  89.4 1.9 divide_convert_fusion
  91.3 9.5 %convolution_convert_fusion = bf16[512,4096]{1,0:T(8,128)(2,1)} fusion(bf16[512,1024]{0,1:T(8,128)(2,1)S(1)} %bitcast.117, bf16[1024,4096]{1,0:T(8,128)(2,1)} %param.13), kind=kOutput, calls=%fused_computation.47 | convolution fusion | flops 4297064448 | bytes 13631488 | tf_op jit(solution)/shard_map/dot_general | solution.py:117
  100.8 88.9 %reduce-scatter.2.cloned.1.call-done = bf16[128,4096]{1,0:T(8,128)(2,1)} async-done(((bf16[512,4096]{1,0:T(8,128)(2,1)}), bf16[128,4096]{1,0:T(8,128)(2,1)}) %reduce-scatter.2.cloned.1.call-update) | async-done | bytes 1048592 | tf_op jit(solution)/shard_map/reduce_scatter | solution.py:116
  (34 shorter events, 7.6 us)
Async XLA Ops:
  6.5 31.1 %copy-start = (s32[128]{0:T(128)S(1)}, s32[128]{0:T(128)}, u32[]{:S(2)}) copy-start(s32[128]{0:T(128)} %param.12) | copy-start | bytes 1540
  8.3 15.3 %all-to-all-start.1 = ((bf16[128,8,128]{0,2,1:T(8,128)(2,1)}), bf16[128,8,128]{0,2,1:T(8,128)(2,1)S(1)}, u32[]{:S(2)}, u32[]{:S(2)}) async-start(bf16[128,8,128]{0,2,1:T(8,128)(2,1)} %bitcast.31), calls=%async_computation.1 | async-start | bytes 524288 | tf_op jit(solution)/shard_map/all_to_all | solution.py:43
  23.6 10.4 %all-to-all-start.2 = ((bf16[128,8,128]{0,2,1:T(8,128)(2,1)}), bf16[128,8,128]{0,2,1:T(8,128)(2,1)S(1)}, u32[]{:S(2)}, u32[]{:S(2)}) async-start(bf16[128,8,128]{0,2,1:T(8,128)(2,1)} %bitcast.36), calls=%async_computation.2 | async-start | bytes 524288 | tf_op jit(solution)/shard_map/all_to_all | solution.py:44
  34.0 44.6 %all-to-all-start = ((bf16[128,32,128]{2,0,1:T(8,128)(2,1)}), bf16[128,32,128]{2,0,1:T(8,128)(2,1)S(1)}, u32[]{:S(2)}, u32[]{:S(2)}) async-start(bf16[128,32,128]{2,0,1:T(8,128)(2,1)} %copy.35), calls=%async_computation | async-start | bytes 2097152 | tf_op jit(solution)/shard_map/all_to_all | solution.py:42
  37.5 152.1 %reduce-scatter.2.cloned.1.call-start = ((), (), s32[]{:S(2)}) async-start(), calls=%async_computation.4 | async-start | bytes 5242880 | tf_op jit(solution)/shard_map/reduce_scatter | solution.py:116
  37.6 18.4 %collective-permute-start = (s32[128]{0:T(128)S(1)}, s32[128]{0:T(128)S(1)}, u32[]{:S(2)}, u32[]{:S(2)}) collective-permute-start(s32[128]{0:T(128)S(1)} %copy-done), channel_id=1, source_target_pairs={{0,1},{1,2},{2,3},{3,0},{4,5},{5,6},{6,7},{7,4},{8,9},{9,10},{10,1... | collective-permute-start | bytes 1544 | tf_op jit(solution)/shard_map/ppermute | solution.py:33
  56.0 5.4 %collective-permute-start.1 = (s32[128]{0:T(128)S(1)}, s32[128]{0:T(128)S(1)}, u32[]{:S(2)}, u32[]{:S(2)}) collective-permute-start(s32[128]{0:T(128)S(1)} %collective-permute-done), channel_id=1, source_target_pairs={{0,1},{1,2},{2,3},{3,0},{4,5},{5,6},{6,7},{7,4},{8,9},{9,10},{10,1... | collective-permute-start | bytes 1544 | tf_op jit(solution)/shard_map/ppermute | solution.py:33
  61.3 5.4 %collective-permute-start.2 = (s32[128]{0:T(128)S(1)}, s32[128]{0:T(128)S(1)}, u32[]{:S(2)}, u32[]{:S(2)}) collective-permute-start(s32[128]{0:T(128)S(1)} %collective-permute-done.1), channel_id=1, source_target_pairs={{0,1},{1,2},{2,3},{3,0},{4,5},{5,6},{6,7},{7,4},{8,9},{9,10},{10,1... | collective-permute-start | bytes 1544 | tf_op jit(solution)/shard_map/ppermute | solution.py:33
  68.5 19.0 %collective-permute-start.4 = (bf16[512,2,128]{2,0,1:T(8,128)(2,1)}, bf16[512,2,128]{2,0,1:T(8,128)(2,1)S(1)}, u32[]{:S(2)}, u32[]{:S(2)}) collective-permute-start(bf16[512,2,128]{2,0,1:T(8,128)(2,1)} %bitcast.35), channel_id=1, source_target_pairs={{0,4},{4,8},{8,12},{12,16},{16,20},{20,24},{24,28},{1,5},{5,9},{9,... | collective-permute-start | bytes 786440 | tf_op jit(solution)/shard_map/ppermute | solution.py:13
  69.8 17.7 %collective-permute-start.5 = (bf16[512,2,128]{2,0,1:T(8,128)(2,1)}, bf16[512,2,128]{2,0,1:T(8,128)(2,1)}, u32[]{:S(2)}, u32[]{:S(2)}) collective-permute-start(bf16[512,2,128]{2,0,1:T(8,128)(2,1)} %bitcast.40), channel_id=1, source_target_pairs={{0,4},{4,8},{8,12},{12,16},{16,20},{20,24},{24,28},{1,5},{5,9},{9,... | collective-permute-start | bytes 786440 | tf_op jit(solution)/shard_map/ppermute | solution.py:13
  74.7 2.1 %collective-permute-start.3 = (bf16[512]{0:T(512)(128)(2,1)S(1)}, bf16[512]{0:T(512)(128)(2,1)S(1)}, u32[]{:S(2)}, u32[]{:S(2)}) collective-permute-start(bf16[512]{0:T(512)(128)(2,1)S(1)} %get-tuple-element.165), channel_id=1, source_target_pairs={{0,4},{4,8},{8,12},{12,16},{16,20},{20,24},{24,28},{1,5},{5,9},{9,... | collective-permute-start | bytes 3080 | tf_op jit(solution)/shard_map/ppermute | solution.py:13
Sparse Core Ops, SparseCore 0:
  100.9 88.7 reduce-scatter.1
